TPU v7x, 32 devices: a whole 2x2x4 slice. The times are simulated.
32 devices in a mesh: rep: 8 (over z, core), tp: 4 (over y, x).
Axes of the slice: x: 2, y: 2, z: 4, core: 2. Of those that a mesh axis runs over, the one named last changes fastest.
Arguments:
- hidden: bfloat16 [32, 4608], P('rep'), may hold values from -6 to 6
- positions: int32 [32], P('rep'), may hold values from 1 to 1023
- key_cache: bfloat16 [32, 16, 1024, 128], P('rep', 'tp'), may hold values from -6 to 6
- value_cache: bfloat16 [32, 16, 1024, 128], P('rep', 'tp'), may hold values from -6 to 6
- norm_gain: float32 [4608], replicated, may hold values from 0.1 to 1.9
- q_proj: bfloat16 [4096, 4608], P(('rep', 'tp')), may hold values from -0.09375 to 0.09375
- k_proj: bfloat16 [2048, 4608], P(('rep', 'tp')), may hold values from -0.09375 to 0.09375
- v_proj: bfloat16 [2048, 4608], P(('rep', 'tp')), may hold values from -0.09375 to 0.09375
- o_proj: bfloat16 [4608, 4096], P(('rep', 'tp')), may hold values from -0.09375 to 0.09375
- post_gain: float32 [4608], P('tp'), may hold values from 0.1 to 1.9
Outputs:
- joined_qkv: bfloat16 [4608, 8192], P(None, 'tp')
- wo_heads: bfloat16 [4096, 4608], P('tp')
- attn_out: bfloat16 [32, 4608], P('rep', 'tp')
All inputs are finite; a program needn't handle non-finite values.
Results may differ from a plain program's by a relative error of at most 0.008.
Values may be sent and summed in bfloat16 or wider, within the bound.
A program may use at most 128 MiB of HBM per device.

v0:
```python
import jax
import jax.numpy as jnp
from jax import lax
from jax.sharding import PartitionSpec as P

score_scale = 144.0 ** (-0.5)
soft_cap = 50.0


def rms_scale(values, gain):
    mean_square = jnp.mean(values * values, axis=-1, keepdims=True)
    return values * lax.rsqrt(mean_square + 1e-06) * gain


def rotate(values, positions):
    half = values.shape[-1] // 2
    freq = 10000.0 ** (-2.0 * jnp.arange(half, dtype=jnp.float32) / values.shape[-1])
    angle = positions.astype(jnp.float32)[:, None] * freq[None, :]
    cosine = jnp.cos(angle)[:, None, :]
    sine = jnp.sin(angle)[:, None, :]
    first = values[..., :half]
    second = values[..., half:]
    return jnp.concatenate(
        [first * cosine - second * sine, second * cosine + first * sine], axis=-1
    )


def body(
    hidden, positions, key_cache, value_cache, norm_gain, q_proj, k_proj, v_proj, o_proj, post_gain
):
    tp_count = lax.axis_size("tp")
    replica_count = lax.axis_size("rep")
    per_tp = replica_count // tp_count
    model_width = hidden.shape[1]
    stacked = (
        lax.all_gather(q_proj[None], "rep", axis=0, tiled=True),
        lax.all_gather(k_proj[None], "rep", axis=0, tiled=True),
        lax.all_gather(v_proj[None], "rep", axis=0, tiled=True),
    )
    shaped = [matrix.reshape((tp_count, per_tp, 1) + matrix.shape[1:]) for matrix in stacked]
    arrived = (
        lax.all_to_all(shaped[0], "tp", split_axis=0, concat_axis=2, tiled=True),
        lax.all_to_all(shaped[1], "tp", split_axis=0, concat_axis=2, tiled=True),
        lax.all_to_all(shaped[2], "tp", split_axis=0, concat_axis=2, tiled=True),
    )
    head_block = [matrix.reshape(-1, model_width) for matrix in arrived]
    joined_block = jnp.transpose(jnp.concatenate(head_block, axis=0))
    split_cols = o_proj.reshape(o_proj.shape[0], tp_count, -1)
    rows_of_group = lax.all_to_all(split_cols, "tp", split_axis=1, concat_axis=0, tiled=True)
    complete_rows = lax.all_gather(rows_of_group, "rep", axis=0, tiled=True)
    out_block = jnp.transpose(complete_rows.reshape(model_width, -1))
    batch, kv_local, length, head_dim = key_cache.shape
    q_width = head_block[0].shape[0]
    kv_width = head_block[1].shape[0]
    q_local = q_width // head_dim
    group = q_local // kv_local
    normed = rms_scale(hidden.astype(jnp.float32), norm_gain).astype(jnp.bfloat16)
    query_key_value_projected = jnp.dot(normed, joined_block, preferred_element_type=jnp.float32)
    query = query_key_value_projected[:, :q_width].reshape(batch, q_local, head_dim)
    keys_new = query_key_value_projected[:, q_width : q_width + kv_width].reshape(
        batch, kv_local, head_dim
    )
    values_new = query_key_value_projected[:, q_width + kv_width :].reshape(
        batch, kv_local, head_dim
    )
    query_rot = rotate(query, positions).astype(jnp.bfloat16)
    rotated_keys = rotate(keys_new, positions).astype(jnp.bfloat16)
    values_rot = values_new.astype(jnp.bfloat16)
    grouped_heads = query_rot.reshape(batch, kv_local, group, head_dim)
    scores = (
        jnp.einsum("bkgd,bkld->bkgl", grouped_heads, key_cache, preferred_element_type=jnp.float32)
        * score_scale
    )
    capped = soft_cap * jnp.tanh(scores / soft_cap)
    valid = jnp.arange(length, dtype=jnp.int32)[None, :] < positions[:, None]
    weight_raw = jnp.where(valid[:, None, None, :], jnp.exp(capped), 0.0)
    self_score = (
        jnp.einsum("juzy,juy->juz", grouped_heads, rotated_keys, preferred_element_type=jnp.float32)
        * score_scale
    )
    self_raw = jnp.exp(soft_cap * jnp.tanh(self_score / soft_cap))
    denom = jnp.sum(weight_raw, axis=-1) + self_raw
    weights = (weight_raw / denom[..., None]).astype(jnp.bfloat16)
    self_weight = (self_raw / denom).astype(jnp.bfloat16)
    attention = jnp.einsum(
        "bkgl,bkld->bkgd", weights, value_cache, preferred_element_type=jnp.float32
    )
    attention = (
        attention
        + self_weight.astype(jnp.float32)[..., None] * values_rot.astype(jnp.float32)[:, :, None, :]
    )
    attention = attention.reshape(batch, q_width).astype(jnp.bfloat16)
    partial_out = jnp.dot(attention, out_block, preferred_element_type=jnp.float32)
    width_local = post_gain.shape[0]
    total = lax.psum(partial_out, "tp")
    multiplier = lax.rsqrt(jnp.mean(total * total, axis=1) + 1e-06)
    share = lax.dynamic_slice_in_dim(total, lax.axis_index("tp") * width_local, width_local, 1)
    result = share * multiplier[:, None] * post_gain
    return (joined_block, out_block, result.astype(jnp.bfloat16))


def solution(mesh):
    in_specs = (
        P("rep", None),
        P("rep"),
        P("rep", "tp", None, None),
        P("rep", "tp", None, None),
        P(),
        P(("rep", "tp"), None),
        P(("rep", "tp"), None),
        P(("rep", "tp"), None),
        P(("rep", "tp"), None),
        P("tp"),
    )
    out_specs = (P(None, "tp"), P("tp", None), P("rep", "tp"))
    return jax.shard_map(body, mesh=mesh, in_specs=in_specs, out_specs=out_specs, check_vma=False)
```

profile of v0, /device:TPU:0, one launch (start us, length us, event | category | flops | bytes accessed | tf_op | source)
XLA Modules:
  0.0 437.0 jit_solution(3041150683269415164)
XLA Ops:
  7.2 0.0 all-gather.14.cloned.1.call-start
  7.2 0.7 all-gather.14.cloned.1.call-update
  7.9 0.0 all-gather.12.cloned.1.call-start
  7.9 0.7 all-gather.12.cloned.1.call-update
  8.6 0.0 all-gather.10.cloned.1.call-start
  8.7 0.7 all-gather.10.cloned.1.call-update
  9.4 0.0 all-gather.8.cloned.1.call-start
  9.4 1.4 copy.53
  10.8 20.6 %all_to_all.63 = bf16[144,4,1024]{2,0,1:T(8,128)(2,1)} all-to-all(bf16[144,4,1024]{2,0,1:T(8,128)(2,1)S(1)} %bitcast.63), channel_id=1, replica_groups=mesh['rep'=8,'tp'=4] {'tp'}, dimensions={1} | all-to-all | bytes 2359296 | tf_op jit(solution)/shard_map/all_to_all | solution.py:49
  31.4 0.0 all-gather.8.cloned.1.call-update
  31.5 32.1 %all-gather.14.cloned.1.call-done = bf16[512,4608]{1,0:T(8,128)(2,1)} async-done(((bf16[64,4608]{1,0:T(8,128)(2,1)}), bf16[512,4608]{1,0:T(8,128)(2,1)}) %all-gather.14.cloned.1.call-update) | async-done | bytes 4718608 | tf_op jit(solution)/shard_map/all_gather | solution.py:38
  63.6 5.0 %all-to-all-start.2 = ((bf16[4,2,1,64,4608]{4,3,1,2,0:T(8,128)(2,1)}), bf16[4,2,1,64,4608]{4,3,1,2,0:T(8,128)(2,1)}, u32[]{:S(2)}, u32[]{:S(2)}) async-start(bf16[4,2,1,64,4608]{4,3,1,2,0:T(8,128)(2,1)} %bitcast.61), calls=%async_computation.2 | async-start | bytes 9437184 | tf_op jit(solution)/shard_map/all_to_all | solution.py:44
  68.5 46.7 %all-gather.12.cloned.1.call-done = bf16[512,4608]{1,0:T(8,128)(2,1)} async-done(((bf16[64,4608]{1,0:T(8,128)(2,1)}), bf16[512,4608]{1,0:T(8,128)(2,1)}) %all-gather.12.cloned.1.call-update) | async-done | bytes 4718608 | tf_op jit(solution)/shard_map/all_gather | solution.py:37
  115.2 7.0 %all-to-all-done.2 = bf16[4,2,1,64,4608]{4,3,1,2,0:T(8,128)(2,1)} async-done(((bf16[4,2,1,64,4608]{4,3,1,2,0:T(8,128)(2,1)}), bf16[4,2,1,64,4608]{4,3,1,2,0:T(8,128)(2,1)}, u32[]{:S(2)}, u32[]{:S(2)}) %all-to-all-start.2) | async-done | bytes 4718624 | tf_op jit(solution)/shard_map/all_to_all | solution.py:44
  122.2 5.0 %all-to-all-start.1 = ((bf16[4,2,1,64,4608]{4,3,1,2,0:T(8,128)(2,1)}), bf16[4,2,1,64,4608]{4,3,1,2,0:T(8,128)(2,1)}, u32[]{:S(2)}, u32[]{:S(2)}) async-start(bf16[4,2,1,64,4608]{4,3,1,2,0:T(8,128)(2,1)} %bitcast.60), calls=%async_computation.1 | async-start | bytes 9437184 | tf_op jit(solution)/shard_map/all_to_all | solution.py:43
  127.3 79.1 %all-gather.10.cloned.1.call-done = bf16[1024,4608]{1,0:T(8,128)(2,1)} async-done(((bf16[128,4608]{1,0:T(8,128)(2,1)}), bf16[1024,4608]{1,0:T(8,128)(2,1)}) %all-gather.10.cloned.1.call-update) | async-done | bytes 9437200 | tf_op jit(solution)/shard_map/all_gather | solution.py:36
  206.4 23.7 %copy.36 = bf16[4,2,1,128,4608]{3,1,4,2,0:T(2,128)(2,1)} copy(bf16[4,2,1,128,4608]{4,3,1,0,2:T(8,128)(2,1)} %bitcast.59) | data formatting | bytes 18874368 | tf_op jit(solution)/shard_map/reshape | solution.py:40
  230.1 0.0 copy-start.2
  230.1 0.0 copy-start
  230.1 0.0 all-to-all-done.1
  230.1 6.0 %all-to-all-start = ((bf16[4,2,1,128,4608]{3,1,4,2,0:T(2,128)(2,1)}), bf16[4,2,1,128,4608]{3,1,4,2,0:T(2,128)(2,1)}, u32[]{:S(2)}, u32[]{:S(2)}) async-start(bf16[4,2,1,128,4608]{3,1,4,2,0:T(2,128)(2,1)} %copy.36), calls=%async_computation | async-start | bytes 18874368 | tf_op jit(solution)/shard_map/all_to_all | solution.py:42
  236.1 0.0 all-reduce.2.cloned.1.call-start
  236.2 0.0 copy-done.2
  236.2 0.0 copy-done
  236.2 0.2 fusion.9
  236.4 0.1 iota_compare_fusion
  236.4 0.1 multiply_cosine_fusion
  236.6 4.9 %copy.41 = bf16[4,2,1,64,4608]{4,3,0,1,2:T(8,128)(2,1)} copy(bf16[4,2,1,64,4608]{4,3,1,2,0:T(8,128)(2,1)} %all-to-all-done.2) | data formatting | bytes 9437184 | tf_op jit(solution)/shard_map/all_to_all | solution.py:44
  241.4 4.9 %copy.39 = bf16[4,2,1,64,4608]{4,3,0,1,2:T(8,128)(2,1)} copy(bf16[4,2,1,64,4608]{4,3,1,2,0:T(8,128)(2,1)} %all-to-all-done.1) | data formatting | bytes 9437184 | tf_op jit(solution)/shard_map/all_to_all | solution.py:43
  246.3 50.7 %all-gather.8.cloned.1.call-done = bf16[4608,1,1024]{2,0,1:T(8,128)(2,1)} async-done(((bf16[576,1,1024]{2,0,1:T(8,128)(2,1)}), bf16[4608,1,1024]{2,0,1:T(8,128)(2,1)}) %all-gather.8.cloned.1.call-update) | async-done | bytes 9437200 | tf_op jit(solution)/shard_map/all_gather | solution.py:50
  297.0 12.6 %copy.44 = bf16[1024,4608]{1,0:T(8,128)(2,1)} copy(bf16[1024,4608]{0,1:T(8,128)(2,1)} %bitcast.52) | data formatting | bytes 18874368
  309.6 30.8 %all-to-all-done = bf16[4,2,1,128,4608]{3,1,4,2,0:T(2,128)(2,1)} async-done(((bf16[4,2,1,128,4608]{3,1,4,2,0:T(2,128)(2,1)}), bf16[4,2,1,128,4608]{3,1,4,2,0:T(2,128)(2,1)}, u32[]{:S(2)}, u32[]{:S(2)}) %all-to-all-start) | async-done | bytes 9437216 | tf_op jit(solution)/shard_map/all_to_all | solution.py:42
  340.5 23.5 %copy.37 = bf16[4,2,1,128,4608]{4,3,0,1,2:T(8,128)(2,1)} copy(bf16[4,2,1,128,4608]{3,1,4,2,0:T(2,128)(2,1)} %all-to-all-done) | data formatting | bytes 18874368 | tf_op jit(solution)/shard_map/all_to_all | solution.py:42
  363.9 0.0 copy-done.3
  363.9 9.2 %fusion.2 = f32[4,2048]{1,0:T(4,128)S(1)} fusion(bf16[512,4608]{1,0:T(8,128)(2,1)} %bitcast.55, bf16[512,4608]{1,0:T(8,128)(2,1)} %bitcast.57, bf16[1024,4608]{1,0:T(8,128)(2,1)} %bitcast.53, bf16[4,4608]{1,0:T(4,128)(2,1)S(1)} %copy-done, f32[4608]{0:T(1024)S(1)} %copy-done.3, f32[4]{0:T(128)S(1)} %add_rsqrt_fusion.1), kind=kOutput, calls=%fused_computation.3 | convolution fusion | flops 132194304 | bytes 18962448 | tf_op jit(solution)/shard_map/dot_general | solution.py:58
  373.2 0.1 subtract_convert_fusion.1
  373.3 0.1 subtract_convert_fusion
  373.4 0.1 maximum_bitcast_fusion
  373.4 0.2 fusion.16
  373.6 3.5 fusion.22
  377.2 2.9 fusion.8
  380.1 6.9 %fusion = f32[4,4608]{1,0:T(4,128)} fusion(bf16[4,1024]{1,0:T(4,128)(2,1)S(1)} %convert_element_type.56, bf16[4608,1,1024]{2,0,1:T(8,128)(2,1)} %all-gather.8.cloned.1.call-done), kind=kOutput, calls=%fused_computation.1 | convolution fusion | flops 37748736 | bytes 9519104 | tf_op jit(solution)/shard_map/dot_general | solution.py:93
  387.0 0.0 all-reduce.2.cloned.1.call-update
  387.0 16.4 %fusion.3 = bf16[4608,2048]{0,1:T(8,128)(2,1)} fusion(bf16[512,4608]{1,0:T(8,128)(2,1)} %bitcast.56, bf16[512,4608]{1,0:T(8,128)(2,1)} %bitcast.58, bf16[1024,4608]{1,0:T(8,128)(2,1)} %bitcast.54), kind=kLoop, calls=%fused_computation.4 | loop fusion | flops 56623104 | bytes 37748736 | tf_op jit(solution)/shard_map/transpose | solution.py:47
  403.4 24.6 %copy.43 = bf16[4608,2048]{1,0:T(8,128)(2,1)} copy(bf16[4608,2048]{0,1:T(8,128)(2,1)} %fusion.3) | data formatting | bytes 37748736
  428.0 1.0 multiply_reduce_fusion
  429.1 0.0 copy-done.1
  429.1 1.4 multiply_convert_fusion
  (15 shorter events, 0.1 us)
Async XLA Ops:
  7.2 56.4 %all-gather.14.cloned.1.call-start = ((), (), s32[]{:S(2)}) async-start(), calls=%async_computation.8 | async-start | bytes 5308416 | tf_op jit(solution)/shard_map/all_gather | solution.py:38
  7.9 107.3 %all-gather.12.cloned.1.call-start = ((), (), s32[]{:S(2)}) async-start(), calls=%async_computation.7 | async-start | bytes 5308416 | tf_op jit(solution)/shard_map/all_gather | solution.py:37
  8.6 197.7 %all-gather.10.cloned.1.call-start = ((), (), s32[]{:S(2)}) async-start(), calls=%async_computation.6 | async-start | bytes 10616832 | tf_op jit(solution)/shard_map/all_gather | solution.py:36
  9.4 287.6 %all-gather.8.cloned.1.call-start = ((), (), s32[]{:S(2)}) async-start(), calls=%async_computation.4 | async-start | bytes 10616832 | tf_op jit(solution)/shard_map/all_gather | solution.py:50
  63.6 58.7 %all-to-all-start.2 = ((bf16[4,2,1,64,4608]{4,3,1,2,0:T(8,128)(2,1)}), bf16[4,2,1,64,4608]{4,3,1,2,0:T(8,128)(2,1)}, u32[]{:S(2)}, u32[]{:S(2)}) async-start(bf16[4,2,1,64,4608]{4,3,1,2,0:T(8,128)(2,1)} %bitcast.61), calls=%async_computation.2 | async-start | bytes 9437184 | tf_op jit(solution)/shard_map/all_to_all | solution.py:44
  122.2 107.9 %all-to-all-start.1 = ((bf16[4,2,1,64,4608]{4,3,1,2,0:T(8,128)(2,1)}), bf16[4,2,1,64,4608]{4,3,1,2,0:T(8,128)(2,1)}, u32[]{:S(2)}, u32[]{:S(2)}) async-start(bf16[4,2,1,64,4608]{4,3,1,2,0:T(8,128)(2,1)} %bitcast.60), calls=%async_computation.1 | async-start | bytes 9437184 | tf_op jit(solution)/shard_map/all_to_all | solution.py:43
  230.1 6.0 %copy-start.2 = (s32[4]{0:T(128)S(1)}, s32[4]{0:T(128)}, u32[]{:S(2)}) copy-start(s32[4]{0:T(128)} %param.11) | copy-start | bytes 52
  230.1 6.1 %copy-start = (bf16[4,4608]{1,0:T(4,128)(2,1)S(1)}, bf16[4,4608]{1,0:T(4,128)(2,1)}, u32[]{:S(2)}) copy-start(bf16[4,4608]{1,0:T(4,128)(2,1)} %param.10) | copy-start | bytes 110596
  230.1 110.3 %all-to-all-start = ((bf16[4,2,1,128,4608]{3,1,4,2,0:T(2,128)(2,1)}), bf16[4,2,1,128,4608]{3,1,4,2,0:T(2,128)(2,1)}, u32[]{:S(2)}, u32[]{:S(2)}) async-start(bf16[4,2,1,128,4608]{3,1,4,2,0:T(2,128)(2,1)} %copy.36), calls=%async_computation | async-start | bytes 18874368 | tf_op jit(solution)/shard_map/all_to_all | solution.py:42
  236.1 191.9 %all-reduce.2.cloned.1.call-start = ((), (), s32[]{:S(2)}) async-start(), calls=%async_computation.5 | async-start | bytes 147456 | tf_op jit(solution)/shard_map/psum | solution.py:95
  309.6 54.3 %copy-start.3 = (f32[4608]{0:T(1024)S(1)}, f32[4608]{0:T(1024)}, u32[]{:S(2)}) copy-start(f32[4608]{0:T(1024)} %param.14) | copy-start | bytes 55300
  403.4 25.7 %copy-start.1 = (f32[1152]{0:T(1024)S(1)}, f32[1152]{0:T(1024)}, u32[]{:S(2)}) copy-start(f32[1152]{0:T(1024)} %param.19) | copy-start | bytes 13828
Sparse Core Ops, SparseCore 0:
  9.6 53.9 all-gather.13
  65.2 49.9 all-gather.11
  116.9 89.4 all-gather.9
  207.9 89.1 all-gather.7
  387.1 38.0 all-reduce.1
where the time goes:
time: 440 us; the launch traced here: 437 us
  waiting for transfers between devices  249 us (57%)
  local copies, waits for them, and re-layouts  95.6 us (22%)
  matrix products  22.7 us (5%)
  blocking collectives  20.6 us (5%)
  other arithmetic  19.4 us (4%)
  starting transfers between devices  16.1 us (4%)
  between operations  13.9 us (3%)
    all_gather x1, waiting for transfers between devices, body(): lax.all_gather(q_proj[None], 'rep', axis=0, tiled=True)  79.1 us
    all_gather x1, waiting for transfers between devices, body(): complete_rows = lax.all_gather(rows_of_group, 'rep', axis=0, tiled=True)  50.7 us
    all_gather x1, waiting for transfers between devices, body(): lax.all_gather(k_proj[None], 'rep', axis=0, tiled=True)  46.7 us
    unnamed x12, local copies, waits for them, and re-layouts  37.2 us
    all_gather x1, waiting for transfers between devices, body(): lax.all_gather(v_proj[None], 'rep', axis=0, tiled=True)  32.1 us
    all_to_all x1, waiting for transfers between devices, body(): lax.all_to_all(shaped[0], 'tp', split_axis=0, concat_axis=2, tiled=True)  30.8 us
    reshape x1, local copies, waits for them, and re-layouts, body(): matrix.reshape((tp_count, per_tp, 1) + matrix.shape[1:])  23.7 us
    all_to_all x1, local copies, waits for them, and re-layouts, body(): lax.all_to_all(shaped[0], 'tp', split_axis=0, concat_axis=2, tiled=True)  23.5 us
  transfers between devices with their start and end apart: 8, of which 6 were waited for; matrix products, arithmetic and copies ran while one was open for 20% of the time, Pallas kernels for 0%

commit v1 on v0

--- a/solution.py
+++ b/solution.py
@@ -39,7 +39,12 @@
     )
     shaped = [matrix.reshape((tp_count, per_tp, 1) + matrix.shape[1:]) for matrix in stacked]
     arrived = (
-        lax.all_to_all(shaped[0], "tp", split_axis=0, concat_axis=2, tiled=True),
+        jnp.concatenate(
+            lax.all_to_all(
+                jnp.stack(jnp.split(shaped[0], lax.axis_size("tp"), axis=0)), "tp", 0, 0
+            ),
+            axis=2,
+        ),
         lax.all_to_all(shaped[1], "tp", split_axis=0, concat_axis=2, tiled=True),
         lax.all_to_all(shaped[2], "tp", split_axis=0, concat_axis=2, tiled=True),
     )

time: 440 us -> 473 us (1.075)
  other arithmetic: 19.4 us -> 39 us
  local copies, waits for them, and re-layouts: 95.6 us -> 105 us
    all_gather x1, waiting for transfers between devices: 50.7 us -> 16.2 us  [body(): complete_rows = lax.all_gather(rows_of_group, 'rep', axis=0, tiled=True)]
    all_to_all x1, waiting for transfers between devices: 30.8 us -> 64.3 us  [body(): lax.all_to_all(jnp.stack(jnp.split(shaped[0], lax.axis_size('tp'), axis=0...]
    all_to_all x1, waiting for transfers between devices: 7.02 us -> 34.1 us  [body(): lax.all_to_all(shaped[2], 'tp', split_axis=0, concat_axis=2, tiled=True)]
    another operation x0 -> x4, local copies, waits for them, and re-layouts: none -> 26.1 us  [body(): jnp.stack(jnp.split(shaped[0], lax.axis_size('tp'), axis=0))]
    reshape x1 -> x0, local copies, waits for them, and re-layouts: 23.7 us -> none  [body(): matrix.reshape((tp_count, per_tp, 1) + matrix.shape[1:])]
    another operation x2 -> x3, other arithmetic: 0.16 us -> 19.7 us  [the longest x1 19.6 us: body(): jnp.stack(jnp.split(shaped[0], lax.axis_size('tp'), axis=0))]
    all_gather x1, waiting for transfers between devices: 46.7 us -> 32.1 us  [body(): lax.all_gather(k_proj[None], 'rep', axis=0, tiled=True)]
    all_gather x1, waiting for transfers between devices: 32.1 us -> 18.4 us  [body(): lax.all_gather(v_proj[None], 'rep', axis=0, tiled=True)]
  transfers between devices with their start and end apart: 8 -> 8, of which waited for: 6 -> 6; matrix products, arithmetic and copies ran while one was open for 20% -> 25% of each run, Pallas kernels for 0% -> 0%
where the time goes in v1:
time: 473 us; the launch traced here: 470 us
  waiting for transfers between devices  253 us (53%)
  local copies, waits for them, and re-layouts  105 us (22%)
  other arithmetic  39 us (8%)
  matrix products  22.7 us (5%)
  blocking collectives  20.6 us (4%)
  starting transfers between devices  15.9 us (3%)
  between operations  13.9 us (3%)
    all_gather x1, waiting for transfers between devices, body(): lax.all_gather(q_proj[None], 'rep', axis=0, tiled=True)  86.2 us
    all_to_all x1, waiting for transfers between devices, body(): lax.all_to_all(jnp.stack(jnp.split(shaped[0], lax.axis_size('tp'), axis=0...  64.3 us
    unnamed x12, local copies, waits for them, and re-layouts  37.3 us
    all_to_all x1, waiting for transfers between devices, body(): lax.all_to_all(shaped[2], 'tp', split_axis=0, concat_axis=2, tiled=True)  34.1 us
    all_gather x1, waiting for transfers between devices, body(): lax.all_gather(k_proj[None], 'rep', axis=0, tiled=True)  32.1 us
    another operation x4, local copies, waits for them, and re-layouts, body(): jnp.stack(jnp.split(shaped[0], lax.axis_size('tp'), axis=0))  26.1 us
    all_to_all x1, local copies, waits for them, and re-layouts, body(): lax.all_to_all(jnp.stack(jnp.split(shaped[0], lax.axis_size('tp'), axis=0...  23.5 us
    all_to_all x1, blocking collectives, body(): lax.all_to_all(split_cols, 'tp', split_axis=1, concat_axis=0, tiled=True)  20.6 us
  transfers between devices with their start and end apart: 8, of which 6 were waited for; matrix products, arithmetic and copies ran while one was open for 25% of the time, Pallas kernels for 0%

profile of v1, /device:TPU:0, one launch (start us, length us, event | category | flops | bytes accessed | tf_op | source)
XLA Modules:
  0.0 470.5 jit_solution(965838015428295386)
XLA Ops:
  7.2 0.0 all-gather.12.cloned.1.call-start
  7.2 0.7 all-gather.12.cloned.1.call-update
  7.9 0.0 all-gather.10.cloned.1.call-start
  7.9 0.7 all-gather.10.cloned.1.call-update
  8.6 0.0 all-gather.14.cloned.1.call-start
  8.7 0.7 all-gather.14.cloned.1.call-update
  9.4 0.0 all-gather.8.cloned.1.call-start
  9.4 1.4 copy.73
  10.8 20.6 %all_to_all.53 = bf16[144,4,1024]{2,0,1:T(8,128)(2,1)} all-to-all(bf16[144,4,1024]{2,0,1:T(8,128)(2,1)S(1)} %bitcast.67), channel_id=1, replica_groups=mesh['rep'=8,'tp'=4] {'tp'}, dimensions={1} | all-to-all | bytes 2359296 | tf_op jit(solution)/shard_map/all_to_all | solution.py:54
  31.4 0.0 all-gather.8.cloned.1.call-update
  31.5 32.1 %all-gather.12.cloned.1.call-done = bf16[512,4608]{1,0:T(8,128)(2,1)} async-done(((bf16[64,4608]{1,0:T(8,128)(2,1)}), bf16[512,4608]{1,0:T(8,128)(2,1)}) %all-gather.12.cloned.1.call-update) | async-done | bytes 4718608 | tf_op jit(solution)/shard_map/all_gather | solution.py:37
  63.6 5.0 %all-to-all-start.1 = ((bf16[4,2,1,64,4608]{4,3,1,2,0:T(8,128)(2,1)}), bf16[4,2,1,64,4608]{4,3,1,2,0:T(8,128)(2,1)}, u32[]{:S(2)}, u32[]{:S(2)}) async-start(bf16[4,2,1,64,4608]{4,3,1,2,0:T(8,128)(2,1)} %bitcast.64), calls=%async_computation.1 | async-start | bytes 9437184 | tf_op jit(solution)/shard_map/all_to_all | solution.py:48
  68.6 86.2 %all-gather.10.cloned.1.call-done = bf16[1024,4608]{1,0:T(8,128)(2,1)} async-done(((bf16[128,4608]{1,0:T(8,128)(2,1)}), bf16[1024,4608]{1,0:T(8,128)(2,1)}) %all-gather.10.cloned.1.call-update) | async-done | bytes 9437200 | tf_op jit(solution)/shard_map/all_gather | solution.py:36
  154.7 6.9 %fusion.22 = (bf16[256,4608]{1,0:T(8,128)(2,1)}, bf16[256,4608]{1,0:T(8,128)(2,1)}, bf16[256,4608]{1,0:T(8,128)(2,1)}, bf16[256,4608]{1,0:T(8,128)(2,1)}) fusion(bf16[1024,4608]{1,0:T(8,128)(2,1)} %all-gather.10.cloned.1.call-done), kind=kLoop, calls=%fused_computation.48 | loop fusion | bytes 18874368 | tf_op jit(solution)/shard_map/split | solution.py:44
  161.6 5.7 %copy.63 = bf16[1,1,2,1,128,4608]{4,2,5,3,1,0:T(2,128)(2,1)S(1)} copy(bf16[1,1,2,1,128,4608]{5,4,2,3,1,0:T(8,128)(2,1)} %bitcast.63) | data formatting | bytes 4718592 | tf_op jit(solution)/shard_map/stack | solution.py:44
  167.3 6.8 %copy.64 = bf16[1,1,2,1,128,4608]{4,2,5,3,1,0:T(2,128)(2,1)} copy(bf16[1,1,2,1,128,4608]{5,4,2,3,1,0:T(8,128)(2,1)} %bitcast.62) | data formatting | bytes 4718592 | tf_op jit(solution)/shard_map/stack | solution.py:44
  174.1 6.8 %copy.65 = bf16[1,1,2,1,128,4608]{4,2,5,3,1,0:T(2,128)(2,1)} copy(bf16[1,1,2,1,128,4608]{5,4,2,3,1,0:T(8,128)(2,1)} %bitcast.61) | data formatting | bytes 4718592 | tf_op jit(solution)/shard_map/stack | solution.py:44
  180.9 6.8 %copy.66 = bf16[1,1,2,1,128,4608]{4,2,5,3,1,0:T(2,128)(2,1)} copy(bf16[1,1,2,1,128,4608]{5,4,2,3,1,0:T(8,128)(2,1)} %bitcast.60) | data formatting | bytes 4718592 | tf_op jit(solution)/shard_map/stack | solution.py:44
  187.7 18.4 %all-gather.14.cloned.1.call-done = bf16[512,4608]{1,0:T(8,128)(2,1)} async-done(((bf16[64,4608]{1,0:T(8,128)(2,1)}), bf16[512,4608]{1,0:T(8,128)(2,1)}) %all-gather.14.cloned.1.call-update) | async-done | bytes 4718608 | tf_op jit(solution)/shard_map/all_gather | solution.py:38
  206.0 5.0 %all-to-all-start.2 = ((bf16[4,2,1,64,4608]{4,3,1,2,0:T(8,128)(2,1)}), bf16[4,2,1,64,4608]{4,3,1,2,0:T(8,128)(2,1)}, u32[]{:S(2)}, u32[]{:S(2)}) async-start(bf16[4,2,1,64,4608]{4,3,1,2,0:T(8,128)(2,1)} %bitcast.65), calls=%async_computation.2 | async-start | bytes 9437184 | tf_op jit(solution)/shard_map/all_to_all | solution.py:49
  211.0 19.6 %pad_maximum_fusion.1 = bf16[4,1,2,1,128,4608]{4,2,5,3,1,0:T(2,128)(2,1)} fusion(bf16[1,1,2,1,128,4608]{4,2,5,3,1,0:T(2,128)(2,1)} %copy.66, bf16[1,1,2,1,128,4608]{4,2,5,3,1,0:T(2,128)(2,1)} %copy.65, bf16[1,1,2,1,128,4608]{4,2,5,3,1,0:T(2,128)(2,1)} %copy.64, bf16[1,1,2,1,128,4608]{4,2,5,3,1,0:T(2,128)(2,1)S(1)} %copy.63), kind=kLoop, calls=%fused_computation.1 | loop fusion | flops 14155776 | bytes 18874368 | tf_op jit(solution)/shard_map/stack | solution.py:44
  230.6 0.0 copy-start.2
  230.6 0.0 copy-start
  230.6 34.1 %all-to-all-done.2 = bf16[4,2,1,64,4608]{4,3,1,2,0:T(8,128)(2,1)} async-done(((bf16[4,2,1,64,4608]{4,3,1,2,0:T(8,128)(2,1)}), bf16[4,2,1,64,4608]{4,3,1,2,0:T(8,128)(2,1)}, u32[]{:S(2)}, u32[]{:S(2)}) %all-to-all-start.2) | async-done | bytes 4718624 | tf_op jit(solution)/shard_map/all_to_all | solution.py:49
  264.7 5.8 %all-to-all-start = ((bf16[4,1,2,1,128,4608]{4,2,5,3,1,0:T(2,128)(2,1)}), bf16[4,1,2,1,128,4608]{4,2,5,3,1,0:T(2,128)(2,1)}, u32[]{:S(2)}, u32[]{:S(2)}) async-start(bf16[4,1,2,1,128,4608]{4,2,5,3,1,0:T(2,128)(2,1)} %pad_maximum_fusion.1), calls=%async_computation | async-start | bytes 18874368 | tf_op jit(solution)/shard_map/all_to_all | solution.py:43
  270.5 0.0 all-reduce.2.cloned.1.call-start
  270.6 0.2 fusion.9
  270.8 0.1 iota_compare_fusion
  270.8 0.1 multiply_cosine_fusion
  271.0 5.0 %copy.55 = bf16[4,2,1,64,4608]{4,3,0,1,2:T(8,128)(2,1)} copy(bf16[4,2,1,64,4608]{4,3,1,2,0:T(8,128)(2,1)} %all-to-all-done.1) | data formatting | bytes 9437184 | tf_op jit(solution)/shard_map/all_to_all | solution.py:48
  276.0 4.9 %copy.57 = bf16[4,2,1,64,4608]{4,3,0,1,2:T(8,128)(2,1)} copy(bf16[4,2,1,64,4608]{4,3,1,2,0:T(8,128)(2,1)} %all-to-all-done.2) | data formatting | bytes 9437184 | tf_op jit(solution)/shard_map/all_to_all | solution.py:49
  280.8 16.2 %all-gather.8.cloned.1.call-done = bf16[4608,1,1024]{2,0,1:T(8,128)(2,1)} async-done(((bf16[576,1,1024]{2,0,1:T(8,128)(2,1)}), bf16[4608,1,1024]{2,0,1:T(8,128)(2,1)}) %all-gather.8.cloned.1.call-update) | async-done | bytes 9437200 | tf_op jit(solution)/shard_map/all_gather | solution.py:55
  297.0 12.6 %copy.60 = bf16[1024,4608]{1,0:T(8,128)(2,1)} copy(bf16[1024,4608]{0,1:T(8,128)(2,1)} %bitcast.53) | data formatting | bytes 18874368
  309.6 64.3 %all-to-all-done = bf16[4,1,2,1,128,4608]{4,2,5,3,1,0:T(2,128)(2,1)} async-done(((bf16[4,1,2,1,128,4608]{4,2,5,3,1,0:T(2,128)(2,1)}), bf16[4,1,2,1,128,4608]{4,2,5,3,1,0:T(2,128)(2,1)}, u32[]{:S(2)}, u32[]{:S(2)}) %all-to-all-start) | async-done | bytes 9437216 | tf_op jit(solution)/shard_map/all_to_all | solution.py:43
  373.9 23.5 %copy.53 = bf16[4,1,2,1,128,4608]{5,4,0,2,3,1:T(8,128)(2,1)} copy(bf16[4,1,2,1,128,4608]{4,2,5,3,1,0:T(2,128)(2,1)} %all-to-all-done) | data formatting | bytes 18874368 | tf_op jit(solution)/shard_map/all_to_all | solution.py:43
  397.4 9.2 %fusion.2 = f32[4,2048]{1,0:T(4,128)S(1)} fusion(bf16[512,4608]{1,0:T(8,128)(2,1)} %bitcast.58, bf16[512,4608]{1,0:T(8,128)(2,1)} %bitcast.56, bf16[1024,4608]{1,0:T(8,128)(2,1)} %bitcast.54, bf16[4,4608]{1,0:T(4,128)(2,1)S(1)} %copy-done, f32[4608]{0:T(1024)S(1)} %copy-done.3, f32[4]{0:T(128)S(1)} %add_rsqrt_fusion.1), kind=kOutput, calls=%fused_computation.4 | convolution fusion | flops 132194304 | bytes 18962448 | tf_op jit(solution)/shard_map/dot_general | solution.py:63
  406.6 0.1 subtract_convert_fusion.1
  406.7 0.1 subtract_convert_fusion
  406.8 0.1 maximum_bitcast_fusion
  406.9 0.2 fusion.16
  407.1 3.5 fusion.23
  410.7 2.9 fusion.8
  413.6 6.9 %fusion = f32[4,4608]{1,0:T(4,128)} fusion(bf16[4,1024]{1,0:T(4,128)(2,1)S(1)} %convert_element_type.56, bf16[4608,1,1024]{2,0,1:T(8,128)(2,1)} %all-gather.8.cloned.1.call-done), kind=kOutput, calls=%fused_computation.2 | convolution fusion | flops 37748736 | bytes 9519104 | tf_op jit(solution)/shard_map/dot_general | solution.py:98
  420.4 0.0 all-reduce.2.cloned.1.call-update
  420.5 16.4 %fusion.3 = bf16[4608,2048]{0,1:T(8,128)(2,1)} fusion(bf16[512,4608]{1,0:T(8,128)(2,1)} %bitcast.59, bf16[512,4608]{1,0:T(8,128)(2,1)} %bitcast.57, bf16[1024,4608]{1,0:T(8,128)(2,1)} %bitcast.55), kind=kLoop, calls=%fused_computation.5 | loop fusion | flops 56623104 | bytes 37748736 | tf_op jit(solution)/shard_map/transpose | solution.py:52
  436.9 24.6 %copy.59 = bf16[4608,2048]{1,0:T(8,128)(2,1)} copy(bf16[4608,2048]{0,1:T(8,128)(2,1)} %fusion.3) | data formatting | bytes 37748736
  461.5 1.0 multiply_reduce_fusion
  462.6 1.4 multiply_convert_fusion
  (20 shorter events, 0.1 us)
Async XLA Ops:
  7.2 56.4 %all-gather.12.cloned.1.call-start = ((), (), s32[]{:S(2)}) async-start(), calls=%async_computation.7 | async-start | bytes 5308416 | tf_op jit(solution)/shard_map/all_gather | solution.py:37
  7.9 146.8 %all-gather.10.cloned.1.call-start = ((), (), s32[]{:S(2)}) async-start(), calls=%async_computation.6 | async-start | bytes 10616832 | tf_op jit(solution)/shard_map/all_gather | solution.py:36
  8.6 197.4 %all-gather.14.cloned.1.call-start = ((), (), s32[]{:S(2)}) async-start(), calls=%async_computation.8 | async-start | bytes 5308416 | tf_op jit(solution)/shard_map/all_gather | solution.py:38
  9.4 287.6 %all-gather.8.cloned.1.call-start = ((), (), s32[]{:S(2)}) async-start(), calls=%async_computation.4 | async-start | bytes 10616832 | tf_op jit(solution)/shard_map/all_gather | solution.py:55
  63.6 142.4 %all-to-all-start.1 = ((bf16[4,2,1,64,4608]{4,3,1,2,0:T(8,128)(2,1)}), bf16[4,2,1,64,4608]{4,3,1,2,0:T(8,128)(2,1)}, u32[]{:S(2)}, u32[]{:S(2)}) async-start(bf16[4,2,1,64,4608]{4,3,1,2,0:T(8,128)(2,1)} %bitcast.64), calls=%async_computation.1 | async-start | bytes 9437184 | tf_op jit(solution)/shard_map/all_to_all | solution.py:48
  206.0 58.7 %all-to-all-start.2 = ((bf16[4,2,1,64,4608]{4,3,1,2,0:T(8,128)(2,1)}), bf16[4,2,1,64,4608]{4,3,1,2,0:T(8,128)(2,1)}, u32[]{:S(2)}, u32[]{:S(2)}) async-start(bf16[4,2,1,64,4608]{4,3,1,2,0:T(8,128)(2,1)} %bitcast.65), calls=%async_computation.2 | async-start | bytes 9437184 | tf_op jit(solution)/shard_map/all_to_all | solution.py:49
  230.6 40.0 %copy-start.2 = (s32[4]{0:T(128)S(1)}, s32[4]{0:T(128)}, u32[]{:S(2)}) copy-start(s32[4]{0:T(128)} %param.11) | copy-start | bytes 52
  230.6 40.0 %copy-start = (bf16[4,4608]{1,0:T(4,128)(2,1)S(1)}, bf16[4,4608]{1,0:T(4,128)(2,1)}, u32[]{:S(2)}) copy-start(bf16[4,4608]{1,0:T(4,128)(2,1)} %param.10) | copy-start | bytes 110596
  264.7 109.2 %all-to-all-start = ((bf16[4,1,2,1,128,4608]{4,2,5,3,1,0:T(2,128)(2,1)}), bf16[4,1,2,1,128,4608]{4,2,5,3,1,0:T(2,128)(2,1)}, u32[]{:S(2)}, u32[]{:S(2)}) async-start(bf16[4,1,2,1,128,4608]{4,2,5,3,1,0:T(2,128)(2,1)} %pad_maximum_fusion.1), calls=%async_computation | async-start | bytes 18874368 | tf_op jit(solution)/shard_map/all_to_all | solution.py:43
  270.5 191.0 %all-reduce.2.cloned.1.call-start = ((), (), s32[]{:S(2)}) async-start(), calls=%async_computation.5 | async-start | bytes 147456 | tf_op jit(solution)/shard_map/psum | solution.py:100
  309.6 87.8 %copy-start.3 = (f32[4608]{0:T(1024)S(1)}, f32[4608]{0:T(1024)}, u32[]{:S(2)}) copy-start(f32[4608]{0:T(1024)} %param.14) | copy-start | bytes 55300
  436.9 25.7 %copy-start.1 = (f32[1152]{0:T(1024)S(1)}, f32[1152]{0:T(1024)}, u32[]{:S(2)}) copy-start(f32[1152]{0:T(1024)} %param.19) | copy-start | bytes 13828
Sparse Core Ops, SparseCore 0:
  9.6 53.9 all-gather.11
  65.2 89.4 all-gather.9
  156.4 49.6 all-gather.13
  207.5 89.4 all-gather.7
  420.6 38.7 all-reduce.1
